TPU v7x, 256 devices: a whole 4x4x8 slice. The times are simulated.
256 devices in a mesh: dp: 8 (over x, core), fsdp: 8 (over z), mp: 4 (over y).
Axes of the slice: x: 4, y: 4, z: 8, core: 2. Of those that a mesh axis runs over, the one named last changes fastest.
Arguments:
- gradients: bfloat16 [64, 12, 2, 256, 1024], P(('dp', 'fsdp'), None, None, None, 'mp'), may hold values from -16 to 16
- master: float32 [12, 2, 256, 1024], P(None, None, ('dp', 'fsdp'), 'mp'), may hold values from -0.375 to 0.375
- teacher: float32 [12, 2, 256, 1024], P(None, None, ('dp', 'fsdp'), 'mp'), may hold values from -0.375 to 0.375
- first_moment: float32 [12, 2, 256, 1024], P(None, None, ('dp', 'fsdp'), 'mp'), may hold values from -2.2888184e-05 to 2.2888184e-05
- second_moment: float32 [12, 2, 256, 1024], P(None, None, ('dp', 'fsdp'), 'mp'), may hold values from 0 to 1, as said below
- layer_rates: float32 [12], replicated, may hold values from 0.02 to 0.2
Outputs:
- master_new: float32 [12, 2, 256, 1024], P(None, None, ('dp', 'fsdp'), 'mp')
- teacher_new: float32 [12, 2, 256, 1024], P(None, None, ('dp', 'fsdp'), 'mp')
- first_new: float32 [12, 2, 256, 1024], P(None, None, ('dp', 'fsdp'), 'mp')
- second_new: float32 [12, 2, 256, 1024], P(None, None, ('dp', 'fsdp'), 'mp')
- student_weights: bfloat16 [12, 2, 256, 1024], P(None, None, None, 'mp')
- teacher_weights: bfloat16 [12, 2, 256, 1024], P(None, None, None, 'mp')
Inputs may be any that keep to these rules, and one draw needn't show every extreme that they name: `second_moment`: every entry is positive.
All inputs are finite; a program needn't handle non-finite values.
Results may differ from a plain program's by a relative error of at most 0.0004.
Values may be sent and summed in bfloat16 or wider, within the bound.
No kernel may reach another device: no remote copies, remote signals or barrier semaphores. Data moves between devices by JAX's collectives and lax.ppermute only.
A program may use at most 64 MiB of HBM per device.

v0:
```python
import jax
import jax.numpy as jnp
from jax import lax
from jax.sharding import Mesh
from jax.sharding import PartitionSpec as P

DP = ("dp_0", "dp_1")
DP_FSDP_MP = ("dp_0", "dp_1", "fsdp", "mp")
DP_FSDP = ("dp_0", "dp_1", "fsdp")
CLIP_NORM = 0.1
BETA_ONE = 0.9
BETA_TWO = 0.999
BIAS_ONE = 1.0 - 0.9**50 * 0.9**50
BIAS_TWO = 1.0 - 0.999**50 * 0.999**50
ADAM_EPS = 1e-08
DECAY = 0.05
EMA_KEEP = 0.95


def cut_along(x, dim, length):
    before, after = (x.shape[:dim], x.shape[dim + 1 :])
    return jnp.moveaxis(x.reshape(*before, length, -1, *after), dim, 0)


def summed_on_arrival(x, axis, dim):
    length = lax.axis_size(axis)
    pieces = lax.all_to_all(cut_along(x, dim, length), axis, 0, 0, tiled=True)
    return jnp.sum(pieces, axis=0)


def by_axis(x, axes):
    for axis in axes:
        x = lax.psum(x, axis)
    return x


def side_by_side(arrays, axis, dim, along):
    ends, at = ([], 0)
    for a in arrays[:-1]:
        at += a.shape[along]
        ends.append(at)
    both = jnp.concatenate(arrays, axis=along)
    return tuple(jnp.split(lax.all_gather(both, axis, axis=dim, tiled=True), ends, axis=along))


def shards(gradients, master, teacher, first_moment, second_moment, layer_rates):
    own_grad = gradients[0].astype(jnp.float32)
    halfway = lax.psum_scatter(own_grad, DP, scatter_dimension=2, tiled=True)
    summed = summed_on_arrival(halfway, "fsdp", 2)
    mean_grad = summed / (lax.axis_size(DP) * lax.axis_size("fsdp"))
    norm_sq = by_axis(jnp.sum(mean_grad * mean_grad), DP_FSDP_MP)
    clip_factor = jnp.minimum(1.0, CLIP_NORM / (jnp.sqrt(norm_sq) + 1e-06))
    clipped = clip_factor * mean_grad
    first_new = BETA_ONE * first_moment + (1.0 - BETA_ONE) * clipped
    second_new = BETA_TWO * second_moment + (1.0 - BETA_TWO) * clipped * clipped
    direction = first_new / BIAS_ONE / (jnp.sqrt(second_new / BIAS_TWO) + ADAM_EPS) + DECAY * master
    layer_rate = layer_rates[:, None, None, None]
    master_new = master - layer_rate * direction
    teacher_new = EMA_KEEP * teacher + (1.0 - EMA_KEEP) * master_new
    student_half = master_new.astype(jnp.bfloat16)
    teacher_half = teacher_new.astype(jnp.bfloat16)
    partial_pair = side_by_side((student_half, teacher_half), "fsdp", 2, 0)
    student_weights, teacher_weights = side_by_side((partial_pair[0], partial_pair[1]), DP, 2, 0)
    return (master_new, teacher_new, first_new, second_new, student_weights, teacher_weights)


def solution(mesh):
    torus = Mesh(
        mesh.devices.reshape(4, 2, mesh.shape["fsdp"], mesh.shape["mp"]),
        ("dp_0", "dp_1", "fsdp", "mp"),
    )
    in_specs = (
        P(DP_FSDP, None, None, None, "mp"),
        P(None, None, DP_FSDP, "mp"),
        P(None, None, DP_FSDP, "mp"),
        P(None, None, DP_FSDP, "mp"),
        P(None, None, DP_FSDP, "mp"),
        P(),
    )
    out_specs = (
        P(None, None, DP_FSDP, "mp"),
        P(None, None, DP_FSDP, "mp"),
        P(None, None, DP_FSDP, "mp"),
        P(None, None, DP_FSDP, "mp"),
        P(None, None, None, "mp"),
        P(None, None, None, "mp"),
    )
    return jax.shard_map(
        shards, mesh=torus, in_specs=in_specs, out_specs=out_specs, check_vma=False
    )
```

profile of v0, /device:TPU:1, one launch (start us, length us, event | category | flops | bytes accessed | tf_op | source)
XLA Modules:
  0.0 220.4 jit_solution(2304604764215183388)
XLA Ops:
  7.2 0.0 reduce-scatter.2.cloned.1.call-start
  7.2 5.3 %bitcast_convert_fusion = f32[12,2,256,256]{3,2,1,0:T(8,128)} fusion(bf16[1,12,2,256,256]{4,3,2,1,0:T(8,128)(2,1)} %param.6), kind=kLoop, calls=%fused_computation | loop fusion | flops 1572864 | bytes 9437184 | tf_op jit(solution)/shard_map/convert_element_type | solution.py:47
  12.5 0.0 reduce-scatter.2.cloned.1.call-update
  12.5 0.0 copy-start.2
  12.6 0.0 copy-start.3
  12.6 0.0 copy-start.4
  12.6 0.0 copy-start.5
  12.6 0.0 copy-start.1
  12.6 0.0 all-gather.2.cloned.1.call-start
  12.7 48.3 %reduce-scatter.2.cloned.1.call-done = f32[12,2,32,256]{3,2,1,0:T(8,128)} async-done(((f32[12,2,256,256]{3,2,1,0:T(8,128)}), f32[12,2,32,256]{3,2,1,0:T(8,128)}) %reduce-scatter.2.cloned.1.call-update) | async-done | bytes 786448 | tf_op jit(solution)/shard_map/reduce_scatter | solution.py:48
  61.0 1.7 copy.36
  62.7 0.2 copy.37
  62.9 27.6 %all_to_all.5 = f32[8,12,2,4,256]{4,3,2,1,0:T(4,128)S(1)} all-to-all(f32[8,12,2,4,256]{4,3,2,1,0:T(4,128)S(1)} %copy.37), channel_id=1, replica_groups=mesh['dp_0'=4,'dp_1'=2,'fsdp'=8,'mp'=4] {'fsdp'}, dimensions={0} | all-to-all | bytes 1572864 | tf_op jit(solution)/shard_map/all_to_all | solution.py:27
  90.5 0.1 reduce_sum.18
  90.6 0.7 multiply_reduce_fusion
  91.3 11.4 %psum.28 = f32[]{:T(128)} all-reduce(f32[]{:T(128)} %multiply_reduce_fusion), channel_id=1, replica_groups=mesh['dp_0'=4,'dp_1'=2,'fsdp'=8,'mp'=4] {'dp_0'}, use_global_device_ids=true, to_apply=%region_3.0 | all-reduce | flops 1 | bytes 8 | tf_op jit(solution)/shard_map/psum | solution.py:33
  102.7 5.2 %psum.29 = f32[]{:T(128)} all-reduce(f32[]{:T(128)} %psum.28), channel_id=1, replica_groups=mesh['dp_0'=4,'dp_1'=2,'fsdp'=8,'mp'=4] {'dp_1'}, use_global_device_ids=true, to_apply=%region_4.0 | all-reduce | flops 1 | bytes 8 | tf_op jit(solution)/shard_map/psum | solution.py:33
  107.9 11.6 %psum.30 = f32[]{:T(128)} all-reduce(f32[]{:T(128)} %psum.29), channel_id=1, replica_groups=mesh['dp_0'=4,'dp_1'=2,'fsdp'=8,'mp'=4] {'fsdp'}, use_global_device_ids=true, to_apply=%region_5.0 | all-reduce | flops 1 | bytes 8 | tf_op jit(solution)/shard_map/psum | solution.py:33
  119.5 9.0 %psum.31 = f32[]{:T(128)} all-reduce(f32[]{:T(128)} %psum.30), channel_id=1, replica_groups=mesh['dp_0'=4,'dp_1'=2,'fsdp'=8,'mp'=4] {'mp'}, use_global_device_ids=true, to_apply=%region_6.0 | all-reduce | flops 1 | bytes 8 | tf_op jit(solution)/shard_map/psum | solution.py:33
  129.3 0.0 copy-done.2
  129.3 0.0 copy-done.3
  129.3 0.0 copy-done.4
  129.3 0.8 fusion.1
  130.1 0.0 copy-done.1
  130.1 0.7 fusion.3
  130.8 0.1 pad_maximum_fusion
  130.9 22.5 %all_gather.6 = bf16[24,2,32,256]{3,0,1,2:T(8,128)(2,1)} all-gather(bf16[24,2,4,256]{3,0,1,2:T(8,128)(2,1)S(1)} %copy.38), channel_id=1, replica_groups=mesh['dp_0'=4,'dp_1'=2,'fsdp'=8,'mp'=4] {'fsdp'}, dimensions={2}, use_global_device_ids=true | all-gather | bytes 884736 | tf_op jit(solution)/shard_map/all_gather | solution.py:43
  153.4 0.0 all-gather.2.cloned.1.call-update
  153.5 48.7 %all-gather.2.cloned.1.call-done = bf16[24,2,256,256]{3,0,1,2:T(8,128)(2,1)} async-done(((bf16[24,2,32,256]{3,0,1,2:T(8,128)(2,1)}), bf16[24,2,256,256]{3,0,1,2:T(8,128)(2,1)}) %all-gather.2.cloned.1.call-update) | async-done | bytes 6291472 | tf_op jit(solution)/shard_map/all_gather | solution.py:43
  202.2 4.5 %fusion.4 = (bf16[12,2,256,256]{3,0,1,2:T(8,128)(2,1)S(1)}, bf16[12,2,256,256]{3,0,1,2:T(8,128)(2,1)S(1)}) fusion(bf16[24,2,256,256]{3,0,1,2:T(8,128)(2,1)} %all-gather.2.cloned.1.call-done), kind=kLoop, calls=%fused_computation.10 | loop fusion | bytes 12582912 | tf_op jit(solution)/shard_map/split | solution.py:43
  206.7 3.5 %copy.40 = bf16[12,2,256,256]{3,2,1,0:T(8,128)(2,1)} copy(bf16[12,2,256,256]{3,0,1,2:T(8,128)(2,1)S(1)} %get-tuple-element.30) | data formatting | bytes 6291456
  210.1 3.5 %copy.39 = bf16[12,2,256,256]{3,2,1,0:T(8,128)(2,1)} copy(bf16[12,2,256,256]{3,0,1,2:T(8,128)(2,1)S(1)} %get-tuple-element.31) | data formatting | bytes 6291456
  (4 shorter events, 0.0 us)
Async XLA Ops:
  7.2 53.8 %reduce-scatter.2.cloned.1.call-start = ((), (), s32[]{:S(2)}) async-start(), calls=%async_computation.2 | async-start | bytes 7077888 | tf_op jit(solution)/shard_map/reduce_scatter | solution.py:48
  12.5 116.7 %copy-start.2 = (f32[12,2,4,256]{3,2,1,0:T(4,128)S(1)}, f32[12,2,4,256]{3,2,1,0:T(4,128)}, u32[]{:S(2)}) copy-start(f32[12,2,4,256]{3,2,1,0:T(4,128)} %param.7) | copy-start | bytes 294916
  12.6 116.7 %copy-start.3 = (f32[12,2,4,256]{3,2,1,0:T(4,128)S(1)}, f32[12,2,4,256]{3,2,1,0:T(4,128)}, u32[]{:S(2)}) copy-start(f32[12,2,4,256]{3,2,1,0:T(4,128)} %param.9) | copy-start | bytes 294916
  12.6 116.7 %copy-start.4 = (f32[12,2,4,256]{3,2,1,0:T(4,128)S(1)}, f32[12,2,4,256]{3,2,1,0:T(4,128)}, u32[]{:S(2)}) copy-start(f32[12,2,4,256]{3,2,1,0:T(4,128)} %param.10) | copy-start | bytes 294916
  12.6 116.7 %copy-start.5 = (f32[12]{0:T(128)S(1)}, f32[12]{0:T(128)}, u32[]{:S(2)}) copy-start(f32[12]{0:T(128)} %param.11) | copy-start | bytes 148
  12.6 117.5 %copy-start.1 = (f32[12,2,4,256]{3,2,1,0:T(4,128)S(1)}, f32[12,2,4,256]{3,2,1,0:T(4,128)}, u32[]{:S(2)}) copy-start(f32[12,2,4,256]{3,2,1,0:T(4,128)} %param.8) | copy-start | bytes 294916
  12.6 189.5 %all-gather.2.cloned.1.call-start = ((), (), s32[]{:S(2)}) async-start(), calls=%async_computation.3 | async-start | bytes 7077888 | tf_op jit(solution)/shard_map/all_gather | solution.py:43
  130.1 76.5 %copy-start = (f32[12,2,4,256]{3,2,1,0:T(4,128)}, f32[12,2,4,256]{3,2,1,0:T(4,128)S(1)}, u32[]{:S(2)}) copy-start(f32[12,2,4,256]{3,2,1,0:T(4,128)S(1)} %get-tuple-element.25) | copy-start | bytes 294916
Sparse Core Ops, SparseCore 0:
  12.7 48.2 reduce-scatter.1
  153.6 48.5 all-gather.1
where the time goes:
time: 221 us; the launch traced here: 220 us
  waiting for transfers between devices  97 us (44%)
  blocking collectives  87.3 us (40%)
  between operations  14.9 us (7%)
  local copies, waits for them, and re-layouts  13.4 us (6%)
  other arithmetic  7.69 us (3%)
    all_gather x1, waiting for transfers between devices, side_by_side(): lax.all_gather(both, axis, axis=dim, tiled=True)  48.7 us
    reduce_scatter x1, waiting for transfers between devices, shards(): halfway = lax.psum_scatter(own_grad, DP, scatter_dimension=2, tiled=True)  48.3 us
    psum x4, blocking collectives, by_axis(): x = lax.psum(x, axis)  37.2 us
    all_to_all x1, blocking collectives, summed_on_arrival(): pieces = lax.all_to_all(cut_along(x, dim, length), axis, 0, 0, tiled=True)  27.6 us
    all_gather x1, blocking collectives, side_by_side(): lax.all_gather(both, axis, axis=dim, tiled=True)  22.5 us
    unnamed x14, local copies, waits for them, and re-layouts  6.99 us
    convert_element_type x1, other arithmetic, shards(): own_grad = gradients[0].astype(jnp.float32)  5.31 us
    split x1, local copies, waits for them, and re-layouts, side_by_side(): jnp.split(lax.all_gather(both, axis, axis=dim, tiled=True), ends, axis=al...  4.48 us
  transfers between devices with their start and end apart: 2, of which 2 were waited for; matrix products, arithmetic and copies ran while one was open for 0% of the time, Pallas kernels for 0%

commit v1 on v0

--- a/solution.py
+++ b/solution.py
@@ -30,7 +30,7 @@
 
 def by_axis(x, axes):
     for axis in axes:
-        x = lax.psum(x, axis)
+        x = jnp.sum(lax.all_gather(x, axis), axis=0)
     return x
 
 

time: 221 us -> 229 us (1.036)
  blocking collectives: 87.3 us -> 54.4 us
  waiting for transfers between devices: 97 us -> 120 us
  local copies, waits for them, and re-layouts: 13.4 us -> 22.3 us
  starting transfers between devices: 0.08 us -> 6.81 us
  other arithmetic: 7.69 us -> 10.1 us
    psum x4 -> x0, blocking collectives: 37.2 us -> none  [by_axis(): x = lax.psum(x, axis)]
    unnamed x0 -> x4, blocking collectives: none -> 32.2 us
    all_to_all x1 -> x0, blocking collectives: 27.6 us -> none  [summed_on_arrival(): pieces = lax.all_to_all(cut_along(x, dim, length), axis, 0, 0, tiled=True)]
    all_to_all x0 -> x1, waiting for transfers between devices: none -> 22.9 us  [summed_on_arrival(): pieces = lax.all_to_all(cut_along(x, dim, length), axis, 0, 0, tiled=True)]
    unnamed x14 -> x34, local copies, waits for them, and re-layouts: 6.99 us -> 15 us
    all_to_all x0 -> x1, starting transfers between devices: none -> 6.73 us  [summed_on_arrival(): pieces = lax.all_to_all(cut_along(x, dim, length), axis, 0, 0, tiled=True)]
    reduce_sum x0 -> x4, other arithmetic: none -> 2.41 us  [by_axis(): x = jnp.sum(lax.all_gather(x, axis), axis=0)]
  transfers between devices with their start and end apart: 2 -> 3, of which waited for: 2 -> 3; matrix products, arithmetic and copies ran while one was open for 0% -> 0% of each run, Pallas kernels for 0% -> 0%
where the time goes in v1:
time: 229 us
  waiting for transfers between devices  120 us (52%)
  blocking collectives  54.4 us (24%)
  local copies, waits for them, and re-layouts  22.3 us (10%)
  between operations  14.9 us (7%)
  other arithmetic  10.1 us (4%)
  starting transfers between devices  6.81 us (3%)
    all_gather x1, waiting for transfers between devices, side_by_side(): lax.all_gather(both, axis, axis=dim, tiled=True)  48.9 us
    reduce_scatter x1, waiting for transfers between devices, shards(): halfway = lax.psum_scatter(own_grad, DP, scatter_dimension=2, tiled=True)  48.3 us
    unnamed x4, blocking collectives  32.2 us
    all_to_all x1, waiting for transfers between devices, summed_on_arrival(): pieces = lax.all_to_all(cut_along(x, dim, length), axis, 0, 0, tiled=True)  22.9 us
    all_gather x1, blocking collectives, side_by_side(): lax.all_gather(both, axis, axis=dim, tiled=True)  22.2 us
    unnamed x34, local copies, waits for them, and re-layouts  15 us
    all_to_all x1, starting transfers between devices, summed_on_arrival(): pieces = lax.all_to_all(cut_along(x, dim, length), axis, 0, 0, tiled=True)  6.73 us
    convert_element_type x1, other arithmetic, shards(): own_grad = gradients[0].astype(jnp.float32)  5.31 us
  transfers between devices with their start and end apart: 3, of which 3 were waited for; matrix products, arithmetic and copies ran while one was open for 0% of the time, Pallas kernels for 0%

profile of v1, /device:TPU:1, one launch (start us, length us, event | category | flops | bytes accessed | tf_op | source)
XLA Modules:
  0.0 228.7 jit_solution(6026501045474592375)
XLA Ops:
  7.2 5.3 %bitcast_convert_fusion = f32[12,2,256,256]{3,2,1,0:T(8,128)} fusion(bf16[1,12,2,256,256]{4,3,2,1,0:T(8,128)(2,1)} %param.6), kind=kLoop, calls=%fused_computation | loop fusion | flops 1572864 | bytes 9437184 | tf_op jit(solution)/shard_map/convert_element_type | solution.py:47
  12.6 48.3 %reduce-scatter.2.cloned.1.call-done = f32[12,2,32,256]{3,2,1,0:T(8,128)} async-done(((f32[12,2,256,256]{3,2,1,0:T(8,128)}), f32[12,2,32,256]{3,2,1,0:T(8,128)}) %reduce-scatter.2.cloned.1.call-update) | async-done | bytes 786448 | tf_op jit(solution)/shard_map/reduce_scatter | solution.py:48
  61.0 1.7 copy.36
  62.7 1.1 copy.37
  63.8 6.7 %all-to-all-start = ((f32[8,12,2,4,256]{4,3,2,1,0:T(4,128)}), f32[8,12,2,4,256]{4,3,2,1,0:T(4,128)S(1)}, u32[]{:S(2)}, u32[]{:S(2)}) async-start(f32[8,12,2,4,256]{4,3,2,1,0:T(4,128)} %copy.37), calls=%async_computation.1 | async-start | bytes 1572864 | tf_op jit(solution)/shard_map/all_to_all | solution.py:27
  70.6 0.6 dynamic-slice
  71.2 22.9 %all-to-all-done = f32[8,12,2,4,256]{4,3,2,1,0:T(4,128)S(1)} async-done(((f32[8,12,2,4,256]{4,3,2,1,0:T(4,128)}), f32[8,12,2,4,256]{4,3,2,1,0:T(4,128)S(1)}, u32[]{:S(2)}, u32[]{:S(2)}) %all-to-all-start) | async-done | bytes 786464 | tf_op jit(solution)/shard_map/all_to_all | solution.py:27
  94.1 0.1 reduce_sum.54
  94.3 0.7 multiply_reduce_fusion
  94.9 1.4 dynamic-update-slice
  96.3 0.6 dynamic-slice.1
  96.9 8.3 %all-reduce = f32[4]{0:T(128)S(1)} all-reduce(f32[4]{0:T(128)S(1)} %dynamic-update-slice), channel_id=1, replica_groups=mesh['dp_0'=4,'dp_1'=2,'fsdp'=8,'mp'=4] {'dp_0'}, use_global_device_ids=true, to_apply=%add | all-reduce | flops 4 | bytes 32
  105.2 0.6 reduce_sum.56
  105.8 1.4 dynamic-update-slice.1
  107.2 0.6 dynamic-slice.2
  107.8 4.6 %all-reduce.1 = f32[2]{0:T(128)S(1)} all-reduce(f32[2]{0:T(128)S(1)} %dynamic-update-slice.1), channel_id=1, replica_groups=mesh['dp_0'=4,'dp_1'=2,'fsdp'=8,'mp'=4] {'dp_1'}, use_global_device_ids=true, to_apply=%add.1 | all-reduce | flops 2 | bytes 16
  112.4 0.6 reduce_sum.57
  113.0 1.4 dynamic-update-slice.2
  114.4 0.6 dynamic-slice.3
  115.0 10.8 %all-reduce.2 = f32[8]{0:T(128)S(1)} all-reduce(f32[8]{0:T(128)S(1)} %dynamic-update-slice.2), channel_id=1, replica_groups=mesh['dp_0'=4,'dp_1'=2,'fsdp'=8,'mp'=4] {'fsdp'}, use_global_device_ids=true, to_apply=%add.2 | all-reduce | flops 8 | bytes 64
  125.8 0.6 reduce_sum.58
  126.4 1.4 dynamic-update-slice.3
  127.8 8.4 %all-reduce.3 = f32[4]{0:T(128)S(1)} all-reduce(f32[4]{0:T(128)S(1)} %dynamic-update-slice.3), channel_id=1, replica_groups=mesh['dp_0'=4,'dp_1'=2,'fsdp'=8,'mp'=4] {'mp'}, use_global_device_ids=true, to_apply=%add.3 | all-reduce | flops 4 | bytes 32
  136.2 0.6 reduce_sum.59
  137.6 0.8 fusion.1
  138.5 0.7 fusion.3
  139.2 0.1 pad_maximum_fusion
  139.3 22.2 %all_gather.38 = bf16[24,2,32,256]{3,0,1,2:T(8,128)(2,1)} all-gather(bf16[24,2,4,256]{3,0,1,2:T(8,128)(2,1)S(1)} %copy.38), channel_id=1, replica_groups=mesh['dp_0'=4,'dp_1'=2,'fsdp'=8,'mp'=4] {'fsdp'}, dimensions={2}, use_global_device_ids=true | all-gather | bytes 884736 | tf_op jit(solution)/shard_map/all_gather | solution.py:43
  161.5 48.9 %all-gather.2.cloned.1.call-done = bf16[24,2,256,256]{3,0,1,2:T(8,128)(2,1)} async-done(((bf16[24,2,32,256]{3,0,1,2:T(8,128)(2,1)}), bf16[24,2,256,256]{3,0,1,2:T(8,128)(2,1)}) %all-gather.2.cloned.1.call-update) | async-done | bytes 6291472 | tf_op jit(solution)/shard_map/all_gather | solution.py:43
  210.4 4.5 %fusion.4 = (bf16[12,2,256,256]{3,0,1,2:T(8,128)(2,1)S(1)}, bf16[12,2,256,256]{3,0,1,2:T(8,128)(2,1)S(1)}) fusion(bf16[24,2,256,256]{3,0,1,2:T(8,128)(2,1)} %all-gather.2.cloned.1.call-done), kind=kLoop, calls=%fused_computation.10 | loop fusion | bytes 12582912 | tf_op jit(solution)/shard_map/split | solution.py:43
  214.9 3.5 %copy.40 = bf16[12,2,256,256]{3,2,1,0:T(8,128)(2,1)} copy(bf16[12,2,256,256]{3,0,1,2:T(8,128)(2,1)S(1)} %get-tuple-element.30) | data formatting | bytes 6291456
  218.4 3.5 %copy.39 = bf16[12,2,256,256]{3,2,1,0:T(8,128)(2,1)} copy(bf16[12,2,256,256]{3,0,1,2:T(8,128)(2,1)S(1)} %get-tuple-element.31) | data formatting | bytes 6291456
  (29 shorter events, 0.2 us)
Async XLA Ops:
  7.2 53.8 %reduce-scatter.2.cloned.1.call-start = ((), (), s32[]{:S(2)}) async-start(), calls=%async_computation.2 | async-start | bytes 7077888 | tf_op jit(solution)/shard_map/reduce_scatter | solution.py:48
  12.5 58.1 %copy-start.9 = (u32[256]{0:T(256)S(1)}, u32[256]{0:T(256)}, u32[]{:S(2)}) copy-start(u32[256]{0:T(256)} %constant.37) | copy-start | bytes 3076
  12.6 83.8 %copy-start.8 = (u32[256]{0:T(256)S(1)}, u32[256]{0:T(256)}, u32[]{:S(2)}) copy-start(u32[256]{0:T(256)} %constant.42) | copy-start | bytes 3076
  12.6 94.6 %copy-start.7 = (u32[256]{0:T(256)S(1)}, u32[256]{0:T(256)}, u32[]{:S(2)}) copy-start(u32[256]{0:T(256)} %constant.47) | copy-start | bytes 3076
  12.6 101.8 %copy-start.6 = (u32[256]{0:T(256)S(1)}, u32[256]{0:T(256)}, u32[]{:S(2)}) copy-start(u32[256]{0:T(256)} %constant.52) | copy-start | bytes 3076
  12.6 125.0 %copy-start.2 = (f32[12,2,4,256]{3,2,1,0:T(4,128)S(1)}, f32[12,2,4,256]{3,2,1,0:T(4,128)}, u32[]{:S(2)}) copy-start(f32[12,2,4,256]{3,2,1,0:T(4,128)} %param.7) | copy-start | bytes 294916
  12.6 125.0 %copy-start.3 = (f32[12,2,4,256]{3,2,1,0:T(4,128)S(1)}, f32[12,2,4,256]{3,2,1,0:T(4,128)}, u32[]{:S(2)}) copy-start(f32[12,2,4,256]{3,2,1,0:T(4,128)} %param.9) | copy-start | bytes 294916
  12.6 125.0 %copy-start.4 = (f32[12,2,4,256]{3,2,1,0:T(4,128)S(1)}, f32[12,2,4,256]{3,2,1,0:T(4,128)}, u32[]{:S(2)}) copy-start(f32[12,2,4,256]{3,2,1,0:T(4,128)} %param.10) | copy-start | bytes 294916
  12.6 125.0 %copy-start.5 = (f32[12]{0:T(128)S(1)}, f32[12]{0:T(128)}, u32[]{:S(2)}) copy-start(f32[12]{0:T(128)} %param.11) | copy-start | bytes 148
  12.6 125.8 %copy-start.1 = (f32[12,2,4,256]{3,2,1,0:T(4,128)S(1)}, f32[12,2,4,256]{3,2,1,0:T(4,128)}, u32[]{:S(2)}) copy-start(f32[12,2,4,256]{3,2,1,0:T(4,128)} %param.8) | copy-start | bytes 294916
  63.8 30.3 %all-to-all-start = ((f32[8,12,2,4,256]{4,3,2,1,0:T(4,128)}), f32[8,12,2,4,256]{4,3,2,1,0:T(4,128)S(1)}, u32[]{:S(2)}, u32[]{:S(2)}) async-start(f32[8,12,2,4,256]{4,3,2,1,0:T(4,128)} %copy.37), calls=%async_computation.1 | async-start | bytes 1572864 | tf_op jit(solution)/shard_map/all_to_all | solution.py:27
  70.5 139.8 %all-gather.2.cloned.1.call-start = ((), (), s32[]{:S(2)}) async-start(), calls=%async_computation.3 | async-start | bytes 7077888 | tf_op jit(solution)/shard_map/all_gather | solution.py:43
  138.5 76.4 %copy-start = (f32[12,2,4,256]{3,2,1,0:T(4,128)}, f32[12,2,4,256]{3,2,1,0:T(4,128)S(1)}, u32[]{:S(2)}) copy-start(f32[12,2,4,256]{3,2,1,0:T(4,128)S(1)} %get-tuple-element.25) | copy-start | bytes 294916
Sparse Core Ops, SparseCore 0:
  12.7 48.2 reduce-scatter.1
  161.6 48.6 all-gather.1
